TPU v7x, 32 devices: a whole 2x2x4 slice. The times are simulated.
32 devices in a mesh: gx: 4 (over z), gy: 4 (over x, core), col: 2 (over y).
Axes of the slice: x: 2, y: 2, z: 4, core: 2. Of those that a mesh axis runs over, the one named last changes fastest.
Arguments:
- fields: bfloat16 [2, 128, 128, 32, 128], P('col', 'gx', 'gy'), may hold values from -6 to 6
- spectral: bfloat16 [1, 16, 16, 2, 32, 32, 16], P(None, 'gx', 'gy', None, None, 'col'), may hold values from -0.75 to 0.75
- skip_weight: bfloat16 [1, 32, 32], replicated, may hold values from -1 to 1
- skip_bias: float32 [1, 32], replicated, may hold values from -3 to 3
- norm_gain: float32 [1, 32], replicated, may hold values from 0.5 to 1.5
- norm_shift: float32 [1, 32], replicated, may hold values from -3 to 3
Outputs:
- activations: bfloat16 [2, 128, 128, 32, 128], P('col', 'gx', 'gy')
All inputs are finite; a program needn't handle non-finite values.
Results may differ from a plain program's by a relative error of at most 0.012.
Values may be sent and summed in bfloat16 or wider, within the bound.
A program may use at most 128 MiB of HBM per device.

v0:
```python
import math
import jax
import jax.numpy as jnp
from jax import lax
from jax.sharding import PartitionSpec as P

X = 128
Y = 128
Z = 128
MX = 16
MY = 16
MZ = 16
norm_eps = 1e-05


def signed_freqs(count):
    index = jnp.arange(count, dtype=jnp.int32)
    return jnp.where(index < count // 2, index, index - count)


def angles(positions, frequency, length):
    turn_count = positions[:, None] * frequency[None, :] % length
    return turn_count.astype(jnp.float32) * (2.0 * math.pi / length)


def forward_table(positions, frequency, length, factor):
    phase_angle = angles(positions, frequency, length)
    cosine = jnp.cos(phase_angle) * factor
    sine_part = jnp.sin(phase_angle) * factor
    from_real = jnp.stack([cosine, -sine_part], axis=-1)
    from_imag = jnp.stack([sine_part, cosine], axis=-1)
    return jnp.stack([from_real, from_imag], axis=1)


def inverse_table(frequency, positions, length):
    phase_angle = angles(positions, frequency, length).T
    cosine = jnp.cos(phase_angle)
    sine_part = jnp.sin(phase_angle)
    from_real = jnp.stack([cosine, sine_part], axis=-1)
    from_imag = jnp.stack([-sine_part, cosine], axis=-1)
    return jnp.stack([from_real, from_imag], axis=1)


def depth_tables(length, count):
    frequency = jnp.arange(count, dtype=jnp.int32)
    phase_angle = angles(jnp.arange(length, dtype=jnp.int32), frequency, length)
    forward = jnp.concatenate([jnp.cos(phase_angle), -jnp.sin(phase_angle)], axis=1)
    backward = jnp.concatenate([jnp.cos(phase_angle).T, -jnp.sin(phase_angle).T], axis=0)
    return (forward.astype(jnp.bfloat16), backward.astype(jnp.bfloat16))


def mix_modes(spectrum, weight):

    def contract(left, right):
        return jnp.einsum("abcz,abcdz->abdz", left, right, preferred_element_type=jnp.float32)

    real_in = spectrum[:, :, :, 0]
    imag_in = spectrum[:, :, :, 1]
    real_weight = weight[:, :, 0]
    imag_weight = weight[:, :, 1]
    real_out = contract(real_in, real_weight) - contract(imag_in, imag_weight)
    imag_out = contract(real_in, imag_weight) + contract(imag_in, real_weight)
    return jnp.stack([real_out, imag_out], axis=3)


def finish(spectral_part, skip_part, offset, scaling, shift_term):
    pre_norm = spectral_part + skip_part + offset[:, None]
    centre = jnp.mean(pre_norm, axis=2, keepdims=True)
    spread = jnp.mean(jnp.square(pre_norm - centre), axis=2, keepdims=True)
    normed = (pre_norm - centre) * lax.rsqrt(spread + norm_eps) * scaling[:, None] + shift_term[
        :, None
    ]
    return jax.nn.gelu(normed, approximate=False).astype(jnp.bfloat16)


def local(fields, spectral, skip_weight, skip_bias, norm_gain, norm_shift):
    highest = lax.Precision.HIGHEST
    hidden = fields[0]
    tile_first, tile_second, channels, depth_cells = hidden.shape
    first_cells = lax.axis_index("gx") * tile_first + jnp.arange(tile_first, dtype=jnp.int32)
    second_cells = lax.axis_index("gy") * tile_second + jnp.arange(tile_second, dtype=jnp.int32)
    depth_forward, depth_backward = depth_tables(Z, MZ)
    second_forward = forward_table(second_cells, signed_freqs(MY), Y, 1.0).astype(jnp.bfloat16)
    first_forward = forward_table(first_cells, signed_freqs(MX), X, 1.0 / math.sqrt(X * Y * Z))
    first_inverse = inverse_table(signed_freqs(MX), first_cells, X).astype(jnp.bfloat16)
    second_inverse = inverse_table(signed_freqs(MY), second_cells, Y)
    inverse_scale = 1.0 / math.sqrt(MX * MY * MZ)
    amplitude = jnp.dot(
        hidden.reshape(-1, depth_cells), depth_forward, preferred_element_type=jnp.float32
    )
    amplitude = amplitude.astype(jnp.bfloat16).reshape(tile_first, tile_second, channels, 2, MZ)
    along_second = jnp.einsum(
        "xycrz,yrks->xkcsz", amplitude, second_forward, preferred_element_type=jnp.float32
    )
    summed_second = lax.psum_scatter(
        along_second.astype(jnp.bfloat16), "gy", scatter_dimension=1, tiled=True
    ).astype(jnp.float32)
    partial_modes = jnp.einsum("xkcsz,xsjt->jkctz", summed_second, first_forward, precision=highest)
    summed = lax.psum_scatter(
        partial_modes.astype(jnp.bfloat16), "gx", scatter_dimension=0, tiled=True
    )
    weights_here = spectral[0]
    mixed_modes = mix_modes(summed, lax.all_gather(weights_here, "col", axis=4, tiled=True)).astype(
        jnp.bfloat16
    )
    gathered_second = lax.all_gather(mixed_modes, "gy", axis=1, tiled=True)
    full_modes = lax.all_gather(gathered_second, "gx", axis=0, tiled=True)
    rows_first = jnp.einsum(
        "jkcsz,jsxt->xkctz", full_modes, first_inverse, preferred_element_type=jnp.float32
    )
    rows_both = jnp.einsum(
        "xkcsz,ksyt->xyctz", rows_first, second_inverse, precision=highest
    ).astype(jnp.bfloat16)
    spectral_part = jnp.dot(
        rows_both.reshape(-1, 2 * MZ), depth_backward, preferred_element_type=jnp.float32
    )
    spectral_part = (
        spectral_part.reshape(tile_first, tile_second, channels, depth_cells) * inverse_scale
    )
    skip_part = jnp.einsum(
        "oc,xycz->xyoz", skip_weight[0], hidden, preferred_element_type=jnp.float32
    )
    hidden = finish(spectral_part, skip_part, skip_bias[0], norm_gain[0], norm_shift[0])
    return hidden[None]


def solution(mesh):
    placed = (
        P("col", "gx", "gy", None, None),
        P(None, "gx", "gy", None, None, "col", None),
        P(),
        P(),
        P(),
        P(),
    )
    return jax.shard_map(
        local,
        mesh=mesh,
        in_specs=placed,
        out_specs=P("col", "gx", "gy", None, None),
        check_vma=False,
    )
```

profile of v0, /device:TPU:0, one launch (start us, length us, event | category | flops | bytes accessed | tf_op | source)
XLA Modules:
  0.0 268.1 jit_solution(5952482807343169716)
XLA Ops:
  7.4 6.4 %fusion = bf16[32768,32]{0,1:T(8,128)(2,1)S(1)} fusion(bf16[32768,128]{1,0:T(8,128)(2,1)} %bitcast.159, bf16[128,16]{0,1:T(8,128)(2,1)S(1)} %get-tuple-element.37, bf16[128,16]{0,1:T(8,128)(2,1)S(1)} %get-tuple-element.38), kind=kOutput, calls=%fused_computation.1 | convolution fusion | flops 269500416 | bytes 10493952 | tf_op jit(solution)/shard_map/dot_general | solution.py:88
  13.8 7.9 %reshape.722 = bf16[32,32,32,2,16]{2,1,0,4,3:T(8,128)(2,1)} reshape(bf16[32768,32]{0,1:T(8,128)(2,1)S(1)} %fusion) | data formatting | bytes 4194304 | tf_op jit(solution)/shard_map/reshape | solution.py:91
  21.9 4.7 %fusion.24 = bf16[32,16,32,2,16]{2,1,4,0,3:T(8,128)(2,1)S(1)} fusion(bf16[32,32,32,2,16]{2,1,0,4,3:T(8,128)(2,1)} %reshape.722, bf16[32,1,16,2]{0,2,1,3:T(8,128)(2,1)S(1)} %get-tuple-element.16, bf16[32,1,16,2]{0,2,1,3:T(8,128)(2,1)S(1)} %get-tuple-element.15), kind=kOutput, calls=%fused_computation.37 | convolution fusion | flops 67641344 | bytes 3149824 | tf_op jit(solution)/shard_map/xycrz,yrks->xkcsz/dot_general | solution.py:92
  26.6 3.1 %copy.26 = bf16[32,16,32,2,16]{2,4,3,0,1:T(8,128)(2,1)} copy(bf16[32,16,32,2,16]{2,1,4,0,3:T(8,128)(2,1)S(1)} %fusion.24) | data formatting | bytes 2097152 | tf_op jit(solution)/shard_map/convert_element_type | solution.py:96
  30.8 15.1 %fusion.13 = f32[32,32,128,32]{2,3,1,0:T(8,128)} fusion(bf16[1,32,32,32,128]{4,3,2,1,0:T(8,128)(2,1)} %param.6, bf16[1,32,32]{2,1,0:T(8,128)(2,1)S(1)} %copy-done), kind=kOutput, calls=%fused_computation.27 | convolution fusion | flops 268435456 | bytes 25167872 | tf_op jit(solution)/shard_map/oc,xycz->xyoz/dot_general | solution.py:120
  46.0 31.2 %reduce-scatter.3.cloned.1.call-done = bf16[32,4,32,2,16]{2,4,3,0,1:T(8,128)(2,1)} async-done(((bf16[32,16,32,2,16]{2,4,3,0,1:T(8,128)(2,1)}), bf16[32,4,32,2,16]{2,4,3,0,1:T(8,128)(2,1)}) %reduce-scatter.3.cloned.1.call-update) | async-done | bytes 262160 | tf_op jit(solution)/shard_map/reduce_scatter | solution.py:95
  77.2 1.9 fusion.30
  79.1 0.9 copy.29
  80.1 11.0 %all-gather.3.cloned.1.call-done = bf16[1,4,4,2,32,32,16]{4,6,5,3,2,1,0:T(8,128)(2,1)} async-done(((bf16[1,4,4,2,32,16,16]{4,6,5,3,2,1,0:T(8,128)(2,1)}), bf16[1,4,4,2,32,32,16]{4,6,5,3,2,1,0:T(8,128)(2,1)}) %all-gather.3.cloned.1.call-update) | async-done | bytes 1048592 | tf_op jit(solution)/shard_map/all_gather | solution.py:103
  91.1 4.5 %slice_bitcast_fusion = (bf16[4,4,32,32,16]{2,4,3,1,0:T(8,128)(2,1)}, bf16[4,4,32,32,16]{2,4,3,1,0:T(8,128)(2,1)S(1)}) fusion(bf16[4,4,2,32,32,16]{3,5,4,2,1,0:T(8,128)(2,1)} %bitcast.161), kind=kLoop, calls=%fused_computation.39 | loop fusion | bytes 2097152 | tf_op jit(solution)/shard_map/squeeze | solution.py:60
  95.6 4.5 %copy.44 = bf16[4,4,32,32,16]{3,2,4,1,0:T(8,128)(2,1)} copy(bf16[4,4,32,32,16]{2,4,3,1,0:T(8,128)(2,1)} %get-tuple-element.5) | data formatting | bytes 1048576 | tf_op jit(solution)/shard_map/squeeze | solution.py:60
  100.2 2.9 %copy.41 = bf16[4,4,32,32,16]{3,2,4,1,0:T(8,128)(2,1)} copy(bf16[4,4,32,32,16]{2,4,3,1,0:T(8,128)(2,1)S(1)} %get-tuple-element.6) | data formatting | bytes 1048576 | tf_op jit(solution)/shard_map/squeeze | solution.py:59
  104.0 2.2 fusion.39
  106.2 2.3 fusion.37
  108.5 2.3 fusion.35
  110.7 2.2 fusion.41
  113.1 7.2 %all_gather.10 = bf16[4,16,32,2,16]{2,4,3,0,1:T(8,128)(2,1)S(1)} all-gather(bf16[4,4,32,2,16]{2,4,3,0,1:T(8,128)(2,1)S(1)} %pad_maximum_fusion), channel_id=1, replica_groups=mesh['gx'=4,'gy'=4,'col'=2] {'gy'}, dimensions={1}, use_global_device_ids=true | all-gather | bytes 163840 | tf_op jit(solution)/shard_map/all_gather | solution.py:106
  120.3 38.6 %all_gather.11 = bf16[16,16,32,2,16]{2,4,3,1,0:T(8,128)(2,1)S(1)} all-gather(bf16[4,16,32,2,16]{2,4,3,1,0:T(8,128)(2,1)S(1)} %copy.30), channel_id=1, replica_groups=mesh['gx'=4,'gy'=4,'col'=2] {'gx'}, dimensions={0}, use_global_device_ids=true | all-gather | bytes 655360 | tf_op jit(solution)/shard_map/all_gather | solution.py:107
  158.8 1.5 convolution_bitcast_fusion
  160.3 22.8 %fusion.12 = bf16[32,32,32,2,16]{2,1,4,0,3:T(8,128)(2,1)} fusion(f32[32,16,32,2,16]{2,0,4,1,3:T(8,128)S(1)} %convolution_bitcast_fusion, f32[16,1,32,2]{2,0,3,1:T(8,128)S(1)} %get-tuple-element.10, f32[16,1,32,2]{2,0,3,1:T(8,128)S(1)} %get-tuple-element.9), kind=kOutput, calls=%fused_computation.26 | convolution fusion | flops 403703808 | bytes 4202496 | tf_op jit(solution)/shard_map/xkcsz,ksyt->xyctz/dot_general | solution.py:111
  183.1 10.5 %copy.34 = bf16[32,32,32,2,16]{2,4,3,1,0:T(8,128)(2,1)} copy(bf16[32,32,32,2,16]{2,1,4,0,3:T(8,128)(2,1)} %fusion.12) | data formatting | bytes 4194304 | tf_op jit(solution)/shard_map/convert_element_type | solution.py:113
  193.6 14.5 %fusion.93 = (f32[32,32,128]{2,1,0:T(8,128)S(1)}, f32[32,32,32,128]{3,2,1,0:T(8,128)}) fusion(f32[32]{0:T(128)S(1)} %bitcast.164, f32[32,32,128,32]{2,3,1,0:T(8,128)} %fusion.13, bf16[32,32,32,32]{2,3,1,0:T(8,128)(2,1)} %bitcast.160, bf16[16,128]{1,0:T(8,128)(2,1)S(1)} %get-tuple-element.41, bf16[16,128]{1,0:T(8,128)(2,1)S(1)} %get-tuple-element.42), kind=kOutput, calls=%fused_computation.167 | convolution fusion | flops 285097984 | bytes 36184192 | tf_op jit(solution)/shard_map/dot_general | solution.py:114
  208.2 10.9 %multiply_reduce_fusion = f32[32,32,128]{2,1,0:T(8,128)S(1)} fusion(f32[32,32,32,128]{3,2,1,0:T(8,128)} %get-tuple-element.36, f32[32,32,128]{2,1,0:T(8,128)S(1)} %broadcast_multiply_fusion), kind=kLoop, calls=%fused_computation.23 | loop fusion | flops 12451840 | bytes 17825792 | tf_op jit(solution)/shard_map/reduce_sum | solution.py:69
  219.2 41.4 %fusion.21 = bf16[1,32,32,32,128]{4,3,2,1,0:T(8,128)(2,1)} fusion(f32[32]{0:T(128)S(1)} %bitcast.162, f32[32]{0:T(128)S(1)} %bitcast.163, f32[32,32,128]{2,1,0:T(8,128)S(1)} %add_rsqrt_fusion, f32[32,32,32,128]{3,2,1,0:T(8,128)} %get-tuple-element.36, f32[32,32,128]{2,1,0:T(8,128)S(1)} %broadcast_multiply_fusion), kind=kLoop, calls=%fused_computation.36 | loop fusion | flops 289406976 | bytes 26214656 | tf_op jit(solution)/shard_map/broadcast_in_dim | solution.py:124
  (34 shorter events, 2.4 us)
Async XLA Ops:
  7.4 23.4 %copy-start = (bf16[1,32,32]{2,1,0:T(8,128)(2,1)S(1)}, bf16[1,32,32]{2,1,0:T(8,128)(2,1)}, u32[]{:S(2)}) copy-start(bf16[1,32,32]{2,1,0:T(8,128)(2,1)} %param.8) | copy-start | bytes 6148
  7.4 69.8 %reduce-scatter.3.cloned.1.call-start = ((), (), s32[]{:S(2)}) async-start(), calls=%async_computation.2 | async-start | bytes 5242880 | tf_op jit(solution)/shard_map/reduce_scatter | solution.py:95
  29.7 61.4 %all-gather.3.cloned.1.call-start = ((), (), s32[]{:S(2)}) async-start(), calls=%async_computation.4 | async-start | bytes 6291456 | tf_op jit(solution)/shard_map/all_gather | solution.py:103
  30.3 72.8 %reduce-scatter.5.cloned.1.call-start = ((), (), s32[]{:S(2)}) async-start(), calls=%async_computation.3 | async-start | bytes 655360 | tf_op jit(solution)/shard_map/reduce_scatter | solution.py:99
  160.3 33.3 %copy-start.4 = (f32[1,32]{1,0:T(1,128)S(1)}, f32[1,32]{1,0:T(1,128)}, u32[]{:S(2)}) copy-start(f32[1,32]{1,0:T(1,128)} %param.9) | copy-start | bytes 388
  208.1 11.1 %copy-start.2 = (f32[1,32]{1,0:T(1,128)S(1)}, f32[1,32]{1,0:T(1,128)}, u32[]{:S(2)}) copy-start(f32[1,32]{1,0:T(1,128)} %param.11) | copy-start | bytes 388
  208.1 11.1 %copy-start.3 = (f32[1,32]{1,0:T(1,128)S(1)}, f32[1,32]{1,0:T(1,128)}, u32[]{:S(2)}) copy-start(f32[1,32]{1,0:T(1,128)} %param.10) | copy-start | bytes 388
  208.2 52.5 %copy-start.1 = (bf16[1,32,32]{2,1,0:T(8,128)(2,1)S(1)}, bf16[1,32,32]{2,1,0:T(8,128)(2,1)}, u32[]{:S(2)}) copy-start(bf16[1,32,32]{2,1,0:T(8,128)(2,1)} %param.8) | copy-start | bytes 6148
Sparse Core Ops, SparseCore 0:
  29.9 47.2 reduce-scatter.2
  80.2 21.8 reduce-scatter.4
Sparse Core Ops, SparseCore 1:
  31.8 59.3 all-gather.2
where the time goes:
time: 269 us; the launch traced here: 268 us
  matrix products  75.9 us (28%)
  other arithmetic  53 us (20%)
  blocking collectives  45.7 us (17%)
  waiting for transfers between devices  42.8 us (16%)
  local copies, waits for them, and re-layouts  35.4 us (13%)
  between operations  15 us (6%)
    broadcast_in_dim x1, other arithmetic, local(): return hidden[None]  41.4 us
    all_gather x1, blocking collectives, local(): full_modes = lax.all_gather(gathered_second, 'gx', axis=0, tiled=True)  38.6 us
    reduce_scatter x1, waiting for transfers between devices, local(): lax.psum_scatter(along_second.astype(jnp.bfloat16), 'gy', scatter_dimensi...  31.2 us
    dot_general x1, matrix products, local(): jnp.einsum('xkcsz,ksyt->xyctz', rows_first, second_inverse, precision=hig...  22.8 us
    dot_general x1, matrix products, local(): jnp.einsum('oc,xycz->xyoz', skip_weight[0], hidden, preferred_element_typ...  15.1 us
    dot_general x1, matrix products, local(): jnp.dot(rows_both.reshape(-1, 2 * MZ), depth_backward, preferred_element_...  14.5 us
    all_gather x1, waiting for transfers between devices, local(): lax.all_gather(weights_here, 'col', axis=4, tiled=True)  11 us
    reduce_sum x1, other arithmetic, finish(): spread = jnp.mean(jnp.square(pre_norm - centre), axis=2, keepdims=True)  10.9 us
  transfers between devices with their start and end apart: 3, of which 2 were waited for; matrix products, arithmetic and copies ran while one was open for 11% of the time, Pallas kernels for 0%

commit v1 on v0

--- a/solution.py
+++ b/solution.py
@@ -11,6 +11,22 @@
 MY = 16
 MZ = 16
 norm_eps = 1e-05
+
+
+def product_in_turn(shard, axis, dim, term):
+    count, place, rows = (lax.axis_size(axis), lax.axis_index(axis), shard.shape[dim])
+    right = [(i, (i + 1) % count) for i in range(count)]
+    left = [(i, (i - 1) % count) for i in range(count)]
+    half = count // 2
+    from_left = from_right = shard
+    running = term(shard, place * rows)
+    for step in range(1, half + 1):
+        from_left = lax.ppermute(from_left, axis, right)
+        if step < count - half:
+            from_right = lax.ppermute(from_right, axis, left)
+            running = running + term(from_right, (place + step) % count * rows)
+        running = running + term(from_left, (place - step) % count * rows)
+    return running
 
 
 def signed_freqs(count):
@@ -104,9 +120,16 @@
         jnp.bfloat16
     )
     gathered_second = lax.all_gather(mixed_modes, "gy", axis=1, tiled=True)
-    full_modes = lax.all_gather(gathered_second, "gx", axis=0, tiled=True)
-    rows_first = jnp.einsum(
-        "jkcsz,jsxt->xkctz", full_modes, first_inverse, preferred_element_type=jnp.float32
+    rows_first = product_in_turn(
+        gathered_second,
+        "gx",
+        0,
+        lambda part, start: jnp.einsum(
+            "jkcsz,jsxt->xkctz",
+            part,
+            lax.dynamic_slice_in_dim(first_inverse, start, part.shape[0], axis=0),
+            preferred_element_type=jnp.float32,
+        ),
     )
     rows_both = jnp.einsum(
         "xkcsz,ksyt->xyctz", rows_first, second_inverse, precision=highest

time: 269 us -> 284 us (1.056); the launches traced: 268 us -> 279 us
  blocking collectives: 45.7 us -> 7.15 us
  waiting for transfers between devices: 42.8 us -> 68.8 us
  matrix products: 75.9 us -> 93.1 us
  starting transfers between devices: 0.27 us -> 5.59 us
    all_gather x1 -> x0, blocking collectives: 38.6 us -> none  [local(): full_modes = lax.all_gather(gathered_second, 'gx', axis=0, tiled=True)]
    ppermute x0 -> x3, waiting for transfers between devices: none -> 26.4 us  [the longest x2 26.4 us: product_in_turn(): from_left = lax.ppermute(from_left, axis, right)]
    dot_general x1 -> x4, matrix products: 1.49 us -> 18.6 us  [local(): jnp.einsum('jkcsz,jsxt->xkctz', part, lax.dynamic_slice_in_dim(first_inve...]
    ppermute x0 -> x3, starting transfers between devices: none -> 5.04 us  [the longest x1 3.37 us: product_in_turn(): from_right = lax.ppermute(from_right, axis, left)]
  transfers between devices with their start and end apart: 3 -> 6, of which waited for: 2 -> 4; matrix products, arithmetic and copies ran while one was open for 11% -> 15% of each run, Pallas kernels for 0% -> 0%
where the time goes in v1:
time: 284 us; the launch traced here: 279 us
  matrix products  93.1 us (33%)
  waiting for transfers between devices  68.8 us (24%)
  other arithmetic  53 us (19%)
  local copies, waits for them, and re-layouts  35.7 us (13%)
  between operations  15.4 us (5%)
  blocking collectives  7.15 us (3%)
  starting transfers between devices  5.59 us (2%)
    broadcast_in_dim x1, other arithmetic, local(): return hidden[None]  41.4 us
    reduce_scatter x1, waiting for transfers between devices, local(): lax.psum_scatter(along_second.astype(jnp.bfloat16), 'gy', scatter_dimensi...  30.7 us
    ppermute x2, waiting for transfers between devices, product_in_turn(): from_left = lax.ppermute(from_left, axis, right)  26.4 us
    dot_general x1, matrix products, local(): jnp.einsum('xkcsz,ksyt->xyctz', rows_first, second_inverse, precision=hig...  22.8 us
    dot_general x4, matrix products, local(): jnp.einsum('jkcsz,jsxt->xkctz', part, lax.dynamic_slice_in_dim(first_inve...  18.6 us
    dot_general x1, matrix products, local(): jnp.einsum('oc,xycz->xyoz', skip_weight[0], hidden, preferred_element_typ...  15.2 us
    dot_general x1, matrix products, local(): jnp.dot(rows_both.reshape(-1, 2 * MZ), depth_backward, preferred_element_...  14.4 us
    all_gather x1, waiting for transfers between devices, local(): lax.all_gather(weights_here, 'col', axis=4, tiled=True)  11 us
  transfers between devices with their start and end apart: 6, of which 4 were waited for; matrix products, arithmetic and copies ran while one was open for 15% of the time, Pallas kernels for 0%

profile of v1, /device:TPU:0, one launch (start us, length us, event | category | flops | bytes accessed | tf_op | source)
XLA Modules:
  0.0 278.6 jit_solution(12082684635463805351)
XLA Ops:
  7.4 6.4 %fusion = bf16[32768,32]{0,1:T(8,128)(2,1)S(1)} fusion(bf16[32768,128]{1,0:T(8,128)(2,1)} %bitcast.198, bf16[128,16]{0,1:T(8,128)(2,1)S(1)} %get-tuple-element.37, bf16[128,16]{0,1:T(8,128)(2,1)S(1)} %get-tuple-element.38), kind=kOutput, calls=%fused_computation.1 | convolution fusion | flops 269500416 | bytes 10493952 | tf_op jit(solution)/shard_map/dot_general | solution.py:104
  13.8 7.9 %reshape.722 = bf16[32,32,32,2,16]{2,1,0,4,3:T(8,128)(2,1)} reshape(bf16[32768,32]{0,1:T(8,128)(2,1)S(1)} %fusion) | data formatting | bytes 4194304 | tf_op jit(solution)/shard_map/reshape | solution.py:107
  21.9 4.7 %fusion.25 = bf16[32,16,32,2,16]{2,1,4,0,3:T(8,128)(2,1)S(1)} fusion(bf16[32,32,32,2,16]{2,1,0,4,3:T(8,128)(2,1)} %reshape.722, bf16[32,1,16,2]{0,2,1,3:T(8,128)(2,1)S(1)} %get-tuple-element.16, bf16[32,1,16,2]{0,2,1,3:T(8,128)(2,1)S(1)} %get-tuple-element.15), kind=kOutput, calls=%fused_computation.41 | convolution fusion | flops 67641344 | bytes 3149824 | tf_op jit(solution)/shard_map/xycrz,yrks->xkcsz/dot_general | solution.py:108
  26.6 3.1 %copy.26 = bf16[32,16,32,2,16]{2,4,3,0,1:T(8,128)(2,1)} copy(bf16[32,16,32,2,16]{2,1,4,0,3:T(8,128)(2,1)S(1)} %fusion.25) | data formatting | bytes 2097152 | tf_op jit(solution)/shard_map/convert_element_type | solution.py:112
  31.2 15.2 %fusion.13 = f32[32,32,128,32]{2,3,1,0:T(8,128)} fusion(bf16[1,32,32,32,128]{4,3,2,1,0:T(8,128)(2,1)} %param.6, bf16[1,32,32]{2,1,0:T(8,128)(2,1)S(1)} %copy-done), kind=kOutput, calls=%fused_computation.27 | convolution fusion | flops 268435456 | bytes 25167872 | tf_op jit(solution)/shard_map/oc,xycz->xyoz/dot_general | solution.py:143
  46.4 30.7 %reduce-scatter.3.cloned.1.call-done = bf16[32,4,32,2,16]{2,4,3,0,1:T(8,128)(2,1)} async-done(((bf16[32,16,32,2,16]{2,4,3,0,1:T(8,128)(2,1)}), bf16[32,4,32,2,16]{2,4,3,0,1:T(8,128)(2,1)}) %reduce-scatter.3.cloned.1.call-update) | async-done | bytes 262160 | tf_op jit(solution)/shard_map/reduce_scatter | solution.py:111
  80.1 11.0 %all-gather.3.cloned.1.call-done = bf16[1,4,4,2,32,32,16]{4,6,5,3,2,1,0:T(8,128)(2,1)} async-done(((bf16[1,4,4,2,32,16,16]{4,6,5,3,2,1,0:T(8,128)(2,1)}), bf16[1,4,4,2,32,32,16]{4,6,5,3,2,1,0:T(8,128)(2,1)}) %all-gather.3.cloned.1.call-update) | async-done | bytes 1048592 | tf_op jit(solution)/shard_map/all_gather | solution.py:119
  91.1 4.5 %slice_bitcast_fusion = (bf16[4,4,32,32,16]{2,4,3,1,0:T(8,128)(2,1)}, bf16[4,4,32,32,16]{2,4,3,1,0:T(8,128)(2,1)S(1)}) fusion(bf16[4,4,2,32,32,16]{3,5,4,2,1,0:T(8,128)(2,1)} %bitcast.200), kind=kLoop, calls=%fused_computation.42 | loop fusion | bytes 2097152 | tf_op jit(solution)/shard_map/squeeze | solution.py:76
  95.6 4.5 %copy.45 = bf16[4,4,32,32,16]{3,2,4,1,0:T(8,128)(2,1)} copy(bf16[4,4,32,32,16]{2,4,3,1,0:T(8,128)(2,1)} %get-tuple-element.5) | data formatting | bytes 1048576 | tf_op jit(solution)/shard_map/squeeze | solution.py:76
  100.2 2.9 %copy.42 = bf16[4,4,32,32,16]{3,2,4,1,0:T(8,128)(2,1)} copy(bf16[4,4,32,32,16]{2,4,3,1,0:T(8,128)(2,1)S(1)} %get-tuple-element.6) | data formatting | bytes 1048576 | tf_op jit(solution)/shard_map/squeeze | solution.py:75
  108.5 2.3 fusion.47
  110.7 2.3 fusion.45
  113.1 7.2 %all_gather.7 = bf16[4,16,32,2,16]{2,4,3,0,1:T(8,128)(2,1)S(1)} all-gather(bf16[4,4,32,2,16]{2,4,3,0,1:T(8,128)(2,1)S(1)} %pad_maximum_fusion), channel_id=1, replica_groups=mesh['gx'=4,'gy'=4,'col'=2] {'gy'}, dimensions={1}, use_global_device_ids=true | all-gather | bytes 163840 | tf_op jit(solution)/shard_map/all_gather | solution.py:122
  120.5 3.4 %collective-permute-start = (bf16[4,16,32,2,16]{2,0,3,4,1:T(4,128)(2,1)S(1)}, bf16[4,16,32,2,16]{2,0,3,4,1:T(4,128)(2,1)S(1)}, u32[]{:S(2)}, u32[]{:S(2)}) collective-permute-start(bf16[4,16,32,2,16]{2,0,3,4,1:T(4,128)(2,1)S(1)} %copy.30), channel_id=1, source_target_pairs={{0,24},{8,0},{16,8},{24,16},{1,25},{9,1},{17,9},{25,17},{2,26},{10... | collective-permute-start | bytes 393224 | tf_op jit(solution)/shard_map/ppermute | solution.py:26
  125.4 22.5 %collective-permute-done.1 = bf16[4,16,32,2,16]{2,0,3,4,1:T(4,128)(2,1)S(1)} collective-permute-done((bf16[4,16,32,2,16]{2,0,3,4,1:T(4,128)(2,1)S(1)}, bf16[4,16,32,2,16]{2,0,3,4,1:T(4,128)(2,1)S(1)}, u32[]{:S(2)}, u32[]{:S(2)}) %collective-permute-start.1) | collective-permute-done | bytes 131104 | tf_op jit(solution)/shard_map/ppermute | solution.py:24
  149.5 4.9 %fusion.33 = f32[32,2,16,32,16,1]{3,0,5,4,2,1:T(8,128)} fusion(bf16[4,16,32,2,16]{2,0,3,4,1:T(4,128)(2,1)S(1)} %collective-permute-done.1, s32[]{:T(128)S(6)} %select_n.148, bf16[16,1,32,2]{2,0,1,3:T(8,128)(2,1)S(1)} %get-tuple-element.14, bf16[16,1,32,2]{2,0,1,3:T(8,128)(2,1)S(1)} %get-tuple-element.13), kind=kOutput, calls=%fused_computation.50 | convolution fusion | flops 8390656 | bytes 2232324 | tf_op jit(solution)/shard_map/jkcsz,jsxt->xkctz/dot_general | solution.py:127
  154.4 4.7 %fusion.35 = f32[32,2,16,32,16,1]{3,0,5,4,2,1:T(8,128)} fusion(bf16[4,16,32,2,16]{2,0,3,4,1:T(4,128)(2,1)S(1)} %collective-permute-done, s32[]{:T(128)S(6)} %select_n.146, bf16[16,1,32,2]{2,0,1,3:T(8,128)(2,1)S(1)} %get-tuple-element.14, bf16[16,1,32,2]{2,0,1,3:T(8,128)(2,1)S(1)} %get-tuple-element.13), kind=kOutput, calls=%fused_computation.52 | convolution fusion | flops 8390656 | bytes 2232324 | tf_op jit(solution)/shard_map/jkcsz,jsxt->xkctz/dot_general | solution.py:127
  159.1 4.0 %collective-permute-done.2 = bf16[4,16,32,2,16]{2,0,3,4,1:T(4,128)(2,1)S(1)} collective-permute-done((bf16[4,16,32,2,16]{2,0,3,4,1:T(4,128)(2,1)S(1)}, bf16[4,16,32,2,16]{2,0,3,4,1:T(4,128)(2,1)S(1)}, u32[]{:S(2)}, u32[]{:S(2)}) %collective-permute-start.2) | collective-permute-done | bytes 131104 | tf_op jit(solution)/shard_map/ppermute | solution.py:24
  163.1 7.6 %fusion.17 = f32[32,16,32,2,16]{2,0,4,1,3:T(8,128)S(1)} fusion(f32[32,2,16,32,16,1]{3,0,5,4,2,1:T(8,128)} %fusion.33, f32[32,2,16,32,16,1]{3,0,5,4,2,1:T(8,128)} %fusion.35, f32[32,2,16,32,16,1]{3,0,5,4,2,1:T(8,128)S(1)} %fusion.37, bf16[4,16,32,2,16]{2,0,3,4,1:T(4,128)(2,1)S(1)} %collective-permute-done.2, s32[]{:T(128)S(6)} %select_n.150, ...), kind=kOutput, calls=%fused_computation.32 | convolution fusion | flops 9963520 | bytes 8523780 | tf_op jit(solution)/shard_map/jkcsz,jsxt->xkctz/dot_general | solution.py:127
  170.7 22.8 %fusion.12 = bf16[32,32,32,2,16]{2,1,4,0,3:T(8,128)(2,1)} fusion(f32[32,16,32,2,16]{2,0,4,1,3:T(8,128)S(1)} %fusion.17, f32[16,1,32,2]{2,0,3,1:T(8,128)S(1)} %get-tuple-element.10, f32[16,1,32,2]{2,0,3,1:T(8,128)S(1)} %get-tuple-element.9), kind=kOutput, calls=%fused_computation.26 | convolution fusion | flops 403703808 | bytes 4202496 | tf_op jit(solution)/shard_map/xkcsz,ksyt->xyctz/dot_general | solution.py:134
  193.4 10.5 %copy.35 = bf16[32,32,32,2,16]{2,4,3,1,0:T(8,128)(2,1)} copy(bf16[32,32,32,2,16]{2,1,4,0,3:T(8,128)(2,1)} %fusion.12) | data formatting | bytes 4194304 | tf_op jit(solution)/shard_map/convert_element_type | solution.py:136
  204.0 14.4 %fusion.117 = (f32[32,32,128]{2,1,0:T(8,128)S(1)}, f32[32,32,32,128]{3,2,1,0:T(8,128)}) fusion(f32[32]{0:T(128)S(1)} %bitcast.203, f32[32,32,128,32]{2,3,1,0:T(8,128)} %fusion.13, bf16[32,32,32,32]{2,3,1,0:T(8,128)(2,1)} %bitcast.199, bf16[16,128]{1,0:T(8,128)(2,1)S(1)} %get-tuple-element.41, bf16[16,128]{1,0:T(8,128)(2,1)S(1)} %get-tuple-element.42), kind=kOutput, calls=%fused_computation.196 | convolution fusion | flops 285097984 | bytes 36184192 | tf_op jit(solution)/shard_map/dot_general | solution.py:137
  218.5 10.9 %multiply_reduce_fusion = f32[32,32,128]{2,1,0:T(8,128)S(1)} fusion(f32[32,32,32,128]{3,2,1,0:T(8,128)} %get-tuple-element.36, f32[32,32,128]{2,1,0:T(8,128)S(1)} %broadcast_multiply_fusion), kind=kLoop, calls=%fused_computation.23 | loop fusion | flops 12451840 | bytes 17825792 | tf_op jit(solution)/shard_map/reduce_sum | solution.py:85
  229.5 41.4 %fusion.22 = bf16[1,32,32,32,128]{4,3,2,1,0:T(8,128)(2,1)} fusion(f32[32]{0:T(128)S(1)} %bitcast.201, f32[32]{0:T(128)S(1)} %bitcast.202, f32[32,32,128]{2,1,0:T(8,128)S(1)} %add_rsqrt_fusion, f32[32,32,32,128]{3,2,1,0:T(8,128)} %get-tuple-element.36, f32[32,32,128]{2,1,0:T(8,128)S(1)} %broadcast_multiply_fusion), kind=kLoop, calls=%fused_computation.40 | loop fusion | flops 289406976 | bytes 26214656 | tf_op jit(solution)/shard_map/broadcast_in_dim | solution.py:147
  (42 shorter events, 13.5 us)
Async XLA Ops:
  7.4 23.8 %copy-start = (bf16[1,32,32]{2,1,0:T(8,128)(2,1)S(1)}, bf16[1,32,32]{2,1,0:T(8,128)(2,1)}, u32[]{:S(2)}) copy-start(bf16[1,32,32]{2,1,0:T(8,128)(2,1)} %param.8) | copy-start | bytes 6148
  7.4 69.8 %reduce-scatter.3.cloned.1.call-start = ((), (), s32[]{:S(2)}) async-start(), calls=%async_computation.2 | async-start | bytes 5242880 | tf_op jit(solution)/shard_map/reduce_scatter | solution.py:111
  29.7 61.4 %all-gather.3.cloned.1.call-start = ((), (), s32[]{:S(2)}) async-start(), calls=%async_computation.4 | async-start | bytes 6291456 | tf_op jit(solution)/shard_map/all_gather | solution.py:119
  30.3 72.8 %reduce-scatter.5.cloned.1.call-start = ((), (), s32[]{:S(2)}) async-start(), calls=%async_computation.3 | async-start | bytes 655360 | tf_op jit(solution)/shard_map/reduce_scatter | solution.py:115
  120.5 33.9 %collective-permute-start = (bf16[4,16,32,2,16]{2,0,3,4,1:T(4,128)(2,1)S(1)}, bf16[4,16,32,2,16]{2,0,3,4,1:T(4,128)(2,1)S(1)}, u32[]{:S(2)}, u32[]{:S(2)}) collective-permute-start(bf16[4,16,32,2,16]{2,0,3,4,1:T(4,128)(2,1)S(1)} %copy.30), channel_id=1, source_target_pairs={{0,24},{8,0},{16,8},{24,16},{1,25},{9,1},{17,9},{25,17},{2,26},{10... | collective-permute-start | bytes 393224 | tf_op jit(solution)/shard_map/ppermute | solution.py:26
  123.9 23.9 %collective-permute-start.1 = (bf16[4,16,32,2,16]{2,0,3,4,1:T(4,128)(2,1)S(1)}, bf16[4,16,32,2,16]{2,0,3,4,1:T(4,128)(2,1)S(1)}, u32[]{:S(2)}, u32[]{:S(2)}) collective-permute-start(bf16[4,16,32,2,16]{2,0,3,4,1:T(4,128)(2,1)S(1)} %copy.30), channel_id=1, source_target_pairs={{0,8},{8,16},{16,24},{24,0},{1,9},{9,17},{17,25},{25,1},{2,10},{10... | collective-permute-start | bytes 393224 | tf_op jit(solution)/shard_map/ppermute | solution.py:24
  147.8 15.3 %collective-permute-start.2 = (bf16[4,16,32,2,16]{2,0,3,4,1:T(4,128)(2,1)S(1)}, bf16[4,16,32,2,16]{2,0,3,4,1:T(4,128)(2,1)S(1)}, u32[]{:S(2)}, u32[]{:S(2)}) collective-permute-start(bf16[4,16,32,2,16]{2,0,3,4,1:T(4,128)(2,1)S(1)} %collective-permute-done.1), channel_id=1, source_target_pairs={{0,8},{8,16},{16,24},{24,0},{1,9},{9,17},{17,25},{25,1},{2,10},{10... | collective-permute-start | bytes 393224 | tf_op jit(solution)/shard_map/ppermute | solution.py:24
  170.7 33.3 %copy-start.4 = (f32[1,32]{1,0:T(1,128)S(1)}, f32[1,32]{1,0:T(1,128)}, u32[]{:S(2)}) copy-start(f32[1,32]{1,0:T(1,128)} %param.9) | copy-start | bytes 388
  218.4 11.1 %copy-start.2 = (f32[1,32]{1,0:T(1,128)S(1)}, f32[1,32]{1,0:T(1,128)}, u32[]{:S(2)}) copy-start(f32[1,32]{1,0:T(1,128)} %param.11) | copy-start | bytes 388
  218.4 11.1 %copy-start.3 = (f32[1,32]{1,0:T(1,128)S(1)}, f32[1,32]{1,0:T(1,128)}, u32[]{:S(2)}) copy-start(f32[1,32]{1,0:T(1,128)} %param.10) | copy-start | bytes 388
  218.5 52.5 %copy-start.1 = (bf16[1,32,32]{2,1,0:T(8,128)(2,1)S(1)}, bf16[1,32,32]{2,1,0:T(8,128)(2,1)}, u32[]{:S(2)}) copy-start(bf16[1,32,32]{2,1,0:T(8,128)(2,1)} %param.8) | copy-start | bytes 6148
Sparse Core Ops, SparseCore 0:
  29.9 47.2 reduce-scatter.2
  80.2 21.8 reduce-scatter.4
Sparse Core Ops, SparseCore 1:
  31.8 59.3 all-gather.2
